TPU v7x, 256 devices: a whole 4x4x8 slice. The times are simulated.
256 devices in a mesh: band: 32 (over z, x_hi, core), dom: 8 (over x_lo, y).
Axes of the slice: x: 4 (x_hi: 2, x_lo: 2; x = x_hi * 2 + x_lo), y: 4, z: 8, core: 2. Of those that a mesh axis runs over, the one named last changes fastest.
Arguments:
- orbitals: bfloat16 [256, 128, 128, 128], P('band', None, 'dom'), may hold values from -6 to 6
- occupations: float32 [256], P('band'), may hold values from 0.25 to 2
Outputs:
- potential: float32 [256, 256, 256], P('band', 'dom')
All inputs are finite; a program needn't handle non-finite values.
Results may differ from a plain program's by a relative error of at most 0.0003.
Values sent between devices are 32-bit elements; how exact they have to be, the bound alone decides.
A program may use at most 64 MiB of HBM per device.

v0:
```python
import jax
import jax.numpy as jnp
from jax import lax
from jax.sharding import PartitionSpec as P

interp_weights = (
    3.0 / 256.0,
    -25.0 / 256.0,
    150.0 / 256.0,
    150.0 / 256.0,
    -25.0 / 256.0,
    3.0 / 256.0,
)
deriv_factors = (4.0 / 5.0, -1.0 / 5.0, 4.0 / 105.0, -1.0 / 280.0)


def split_up(value, dim, devices):
    before, after = (value.shape[:dim], value.shape[dim + 1 :])
    return jnp.moveaxis(value.reshape(*before, devices, -1, *after), dim, 0)


def sent_and_summed(value, axis, dim):
    blocks = split_up(value, dim, lax.axis_size(axis))
    arrived = lax.all_to_all(blocks, axis, split_axis=0, concat_axis=0, tiled=True)
    return arrived.sum(axis=0)


def padded_2(value, sides, width):
    for axis, dim in sides:
        devices, length = (lax.axis_size(axis), value.shape[dim])
        up = [(i, (i + 1) % devices) for i in range(devices)]
        down = [(j, i) for i, j in up]
        last = lax.slice_in_dim(value, length - width, length, axis=dim)
        initial = lax.slice_in_dim(value, 0, width, axis=dim)
        before = lax.ppermute(last, axis, up)
        after = lax.ppermute(initial, axis, down)
        value = jnp.concatenate([before, value, after], axis=dim)
    return value


def alternate(even_cells, odd_cells, along):
    stacked = jnp.stack([even_cells, odd_cells], axis=along + 1)
    target_shape = list(even_cells.shape)
    target_shape[along] = 2 * even_cells.shape[along]
    return stacked.reshape(target_shape)


def refine(padded, along, extent):
    odd_cells = jnp.zeros_like(lax.slice_in_dim(padded, 3, 3 + extent, axis=along))
    for offset, factor in zip(range(-2, 4), interp_weights):
        odd_cells = odd_cells + factor * lax.slice_in_dim(
            padded, 3 + offset, 3 + offset + extent, axis=along
        )
    even_cells = lax.slice_in_dim(padded, 3, 3 + extent, axis=along)
    return alternate(even_cells, odd_cells, along)


def wrap_third(field, margin):
    extent = field.shape[2]
    return jnp.concatenate([field[:, :, extent - margin :], field, field[:, :, :margin]], axis=2)


def central(padded, along, start_a, start_b, extent_a, extent_b):
    window_base = padded[start_a : start_a + extent_a, start_b : start_b + extent_b]
    summed = jnp.zeros_like(window_base)
    for offset, factor in zip((1, 2, 3, 4), deriv_factors):
        if along == 0:
            ahead_part = padded[
                start_a + offset : start_a + offset + extent_a, start_b : start_b + extent_b
            ]
            behind_part = padded[
                start_a - offset : start_a - offset + extent_a, start_b : start_b + extent_b
            ]
        elif along == 1:
            ahead_part = padded[
                start_a : start_a + extent_a, start_b + offset : start_b + offset + extent_b
            ]
            behind_part = padded[
                start_a : start_a + extent_a, start_b - offset : start_b - offset + extent_b
            ]
        else:
            ahead_part = jnp.roll(window_base, -offset, 2)
            behind_part = jnp.roll(window_base, offset, 2)
        summed = summed + factor * (ahead_part - behind_part)
    return summed


def pointwise(density, grad_a, grad_b, grad_c):
    shifted = density * density + 0.01
    scaling = 0.01 * shifted ** (4.0 / 3.0)
    reduced = (grad_a * grad_a + grad_b * grad_b + grad_c * grad_c) / scaling
    divisor = 1.0 + 0.2195 * reduced / 0.804
    enhance = 0.804 - 0.804 / divisor
    flux_weight = 0.2195 / (divisor * divisor) / scaling
    local_part = -0.75 * shifted ** (1.0 / 6.0) * (1.0 + enhance)
    return (local_part, flux_weight * grad_a, flux_weight * grad_b, flux_weight * grad_c)


def deep_tail(deep, extent_a, extent_b):
    wider_a, wider_b = (extent_a + 8, extent_b + 8)
    grad_a = central(deep, 0, 4, 4, wider_a, wider_b)
    grad_b = central(deep, 1, 4, 4, wider_a, wider_b)
    grad_c = central(deep, 2, 4, 4, wider_a, wider_b)
    local_part, flux_a, flux_b, flux_c = pointwise(
        deep[4 : 4 + wider_a, 4 : 4 + wider_b], grad_a, grad_b, grad_c
    )
    div_a = central(flux_a, 0, 4, 4, extent_a, extent_b)
    div_b = central(flux_b, 1, 4, 4, extent_a, extent_b)
    div_c = central(flux_c, 2, 4, 4, extent_a, extent_b)
    local_part = local_part[4 : 4 + extent_a, 4 : 4 + extent_b]
    return local_part + 0.2 * (div_a + div_b + div_c)


def on_device(orbitals, occupations):
    weights = occupations / (occupations.shape[0] * lax.axis_size("band"))
    density = sent_and_summed(
        jnp.sum(weights[:, None, None, None] * jnp.square(orbitals.astype(jnp.float32)), axis=0),
        "band",
        0,
    )
    cells_a, cells_b = (density.shape[0], density.shape[1])
    padded = padded_2(density, (("band", 0), ("dom", 1)), 3)
    extent_a, extent_b = (2 * cells_a, 2 * cells_b)
    fine = refine(padded, 0, cells_a)
    fine = refine(fine, 1, cells_b)
    fine = refine(wrap_third(fine, 3), 2, density.shape[2])
    deep = padded_2(fine, (("band", 0), ("dom", 1)), 8)
    return deep_tail(deep, extent_a, extent_b)


def solution(mesh):
    return jax.shard_map(
        on_device,
        mesh=mesh,
        in_specs=(P("band", None, "dom", None), P("band")),
        out_specs=P("band", "dom", None),
        check_vma=False,
    )
```

profile of v0, /device:TPU:24, one launch (start us, length us, event | category | flops | bytes accessed | tf_op | source)
XLA Modules:
  0.0 90.0 jit_solution(7273097623352359899)
XLA Ops:
  0.0 0.7 broadcast_multiply_fusion
  0.7 3.4 %multiply_reduce_fusion = f32[128,16,128]{2,1,0:T(8,128)S(1)} fusion(bf16[8,128,16,128]{3,2,1,0:T(8,128)(2,1)} %param.2, f32[8]{0:T(128)S(1)} %broadcast_multiply_fusion), kind=kLoop, calls=%fused_computation | loop fusion | flops 8126464 | bytes 5242912 | tf_op jit(solution)/shard_map/reduce_sum | solution.py:117
  4.1 39.7 %all_to_all.5 = f32[32,4,16,128]{3,2,1,0:T(8,128)S(1)} all-to-all(f32[32,4,16,128]{3,2,1,0:T(8,128)S(1)} %bitcast.16), channel_id=1, replica_groups=mesh['band'=32,'dom'=8] {'band'}, dimensions={0} | all-to-all | bytes 2097152 | tf_op jit(solution)/shard_map/all_to_all | solution.py:24
  43.9 5.3 %collective-permute-start.1 = (f32[3,16,128]{2,1,0:T(8,128)S(1)}, f32[3,16,128]{2,1,0:T(8,128)S(1)}, u32[]{:S(2)}, u32[]{:S(2)}) collective-permute-start(f32[3,16,128]{2,1,0:T(8,128)S(1)} %get-tuple-element.55), channel_id=1, source_target_pairs={{8,0},{16,8},{24,16},{32,24},{40,32},{48,40},{56,48},{64,56},{72,6... | collective-permute-start | bytes 73736 | tf_op jit(solution)/shard_map/ppermute | solution.py:36
  49.3 1.5 %collective-permute-done = f32[3,16,128]{2,1,0:T(8,128)S(1)} collective-permute-done((f32[3,16,128]{2,1,0:T(8,128)S(1)}, f32[3,16,128]{2,1,0:T(8,128)S(1)}, u32[]{:S(2)}, u32[]{:S(2)}) %collective-permute-start) | collective-permute-done | bytes 24608 | tf_op jit(solution)/shard_map/ppermute | solution.py:35
  50.8 0.3 collective-permute-start.2
  51.2 1.8 %collective-permute-start.3 = (f32[10,3,128]{2,1,0:T(4,128)S(1)}, f32[10,3,128]{2,1,0:T(4,128)S(1)}, u32[]{:S(2)}, u32[]{:S(2)}) collective-permute-start(f32[10,3,128]{2,1,0:T(4,128)S(1)} %get-tuple-element.53), channel_id=1, source_target_pairs={{1,0},{2,1},{3,2},{4,3},{5,4},{6,5},{7,6},{0,7},{9,8},{10,9},{11,1... | collective-permute-start | bytes 46088 | tf_op jit(solution)/shard_map/ppermute | solution.py:36
  52.9 1.8 %collective-permute-done.2 = f32[10,3,128]{2,1,0:T(4,128)S(1)} collective-permute-done((f32[10,3,128]{2,1,0:T(4,128)S(1)}, f32[10,3,128]{2,1,0:T(4,128)S(1)}, u32[]{:S(2)}, u32[]{:S(2)}) %collective-permute-start.2) | collective-permute-done | bytes 15392 | tf_op jit(solution)/shard_map/ppermute | solution.py:35
  54.7 2.4 %collective-permute-done.3 = f32[10,3,128]{2,1,0:T(4,128)S(1)} collective-permute-done((f32[10,3,128]{2,1,0:T(4,128)S(1)}, f32[10,3,128]{2,1,0:T(4,128)S(1)}, u32[]{:S(2)}, u32[]{:S(2)}) %collective-permute-start.3) | collective-permute-done | bytes 15392 | tf_op jit(solution)/shard_map/ppermute | solution.py:36
  57.4 0.4 fusion.58
  57.8 0.5 copy.50
  58.3 0.4 copy.51
  58.7 4.6 %collective-permute-start.5 = (f32[8,32,256]{2,1,0:T(8,128)S(1)}, f32[8,32,256]{2,1,0:T(8,128)S(1)}, u32[]{:S(2)}, u32[]{:S(2)}) collective-permute-start(f32[8,32,256]{2,1,0:T(8,128)S(1)} %copy.51), channel_id=1, source_target_pairs={{8,0},{16,8},{24,16},{32,24},{40,32},{48,40},{56,48},{64,56},{72,6... | collective-permute-start | bytes 786440 | tf_op jit(solution)/shard_map/ppermute | solution.py:36
  63.3 3.9 %collective-permute-done.5 = f32[8,32,256]{2,1,0:T(8,128)S(1)} collective-permute-done((f32[8,32,256]{2,1,0:T(8,128)S(1)}, f32[8,32,256]{2,1,0:T(8,128)S(1)}, u32[]{:S(2)}, u32[]{:S(2)}) %collective-permute-start.5) | collective-permute-done | bytes 262176 | tf_op jit(solution)/shard_map/ppermute | solution.py:36
  67.2 5.6 %collective-permute-done.4 = f32[8,32,256]{2,1,0:T(8,128)S(1)} collective-permute-done((f32[8,32,256]{2,1,0:T(8,128)S(1)}, f32[8,32,256]{2,1,0:T(8,128)S(1)}, u32[]{:S(2)}, u32[]{:S(2)}) %collective-permute-start.4) | collective-permute-done | bytes 262176 | tf_op jit(solution)/shard_map/ppermute | solution.py:35
  72.9 2.0 %collective-permute-start.7 = (f32[24,8,256]{2,1,0:T(8,128)S(1)}, f32[24,8,256]{2,1,0:T(8,128)S(1)}, u32[]{:S(2)}, u32[]{:S(2)}) collective-permute-start(f32[24,8,256]{2,1,0:T(8,128)S(1)} %get-tuple-element.29), channel_id=1, source_target_pairs={{1,0},{2,1},{3,2},{4,3},{5,4},{6,5},{7,6},{0,7},{9,8},{10,9},{11,1... | collective-permute-start | bytes 589832 | tf_op jit(solution)/shard_map/ppermute | solution.py:36
  74.9 3.6 %collective-permute-done.6 = f32[24,8,256]{2,1,0:T(8,128)S(1)} collective-permute-done((f32[24,8,256]{2,1,0:T(8,128)S(1)}, f32[24,8,256]{2,1,0:T(8,128)S(1)}, u32[]{:S(2)}, u32[]{:S(2)}) %collective-permute-start.6) | collective-permute-done | bytes 196640 | tf_op jit(solution)/shard_map/ppermute | solution.py:35
  78.5 2.4 %collective-permute-done.7 = f32[24,8,256]{2,1,0:T(8,128)S(1)} collective-permute-done((f32[24,8,256]{2,1,0:T(8,128)S(1)}, f32[24,8,256]{2,1,0:T(8,128)S(1)}, u32[]{:S(2)}, u32[]{:S(2)}) %collective-permute-start.7) | collective-permute-done | bytes 196640 | tf_op jit(solution)/shard_map/ppermute | solution.py:36
  81.7 0.2 fusion.85
  81.9 0.2 fusion.87
  82.4 0.2 fusion.89
  82.7 3.7 %fusion.77 = (f32[16,40,256]{2,1,0:T(8,128)S(1)}, f32[16,40,256]{2,1,0:T(8,128)S(1)}, f32[16,40,256]{2,1,0:T(8,128)S(1)}, f32[16,40,256]{2,1,0:T(8,128)S(1)}) fusion(f32[24,48,256]{2,1,0:T(8,128)S(1)} %pad_maximum_fusion, f32[8,32,256]{2,1,0:T(8,128)S(1)} %collective-permute-done.5, f32[8,32,256]{2,1,0:T(8,128)S(1)} %copy.51, ...), kind=kLoop, calls=%fused_computation.145 | loop fusion | flops 10158080 | bytes 18874368 | tf_op jit(solution)/shard_map/mul | solution.py:96
  87.4 0.9 fusion.79
  88.3 1.7 %fusion.28 = f32[8,32,256]{2,1,0:T(8,128)} fusion(f32[16,40,256]{2,1,0:T(8,128)S(1)} %get-tuple-element.10, f32[16,40,256]{2,1,0:T(8,128)S(1)} %get-tuple-element.9, f32[16,40,256]{2,1,0:T(8,128)S(1)} %get-tuple-element.6, f32[16,40,256]{2,1,0:T(8,128)S(1)} %get-tuple-element.11, f32[8,32,1]{2,1,0:T(8,128)S(1)} %get-tuple-element.43, ...), kind=kLoop, calls=%fused_computation.56 | loop fusion | flops 3211264 | bytes 7077888 | tf_op jit(solution)/shard_map/add | solution.py:111
  (31 shorter events, 2.5 us)
Async XLA Ops:
  43.9 6.9 %collective-permute-start = (f32[3,16,128]{2,1,0:T(8,128)S(1)}, f32[3,16,128]{2,1,0:T(8,128)S(1)}, u32[]{:S(2)}, u32[]{:S(2)}) collective-permute-start(f32[3,16,128]{2,1,0:T(8,128)S(1)} %get-tuple-element.54), channel_id=1, source_target_pairs={{0,8},{8,16},{16,24},{24,32},{32,40},{40,48},{48,56},{56,64},{64,7... | collective-permute-start | bytes 73736 | tf_op jit(solution)/shard_map/ppermute | solution.py:35
  43.9 6.9 %collective-permute-start.1 = (f32[3,16,128]{2,1,0:T(8,128)S(1)}, f32[3,16,128]{2,1,0:T(8,128)S(1)}, u32[]{:S(2)}, u32[]{:S(2)}) collective-permute-start(f32[3,16,128]{2,1,0:T(8,128)S(1)} %get-tuple-element.55), channel_id=1, source_target_pairs={{8,0},{16,8},{24,16},{32,24},{40,32},{48,40},{56,48},{64,56},{72,6... | collective-permute-start | bytes 73736 | tf_op jit(solution)/shard_map/ppermute | solution.py:36
  50.8 3.9 %collective-permute-start.2 = (f32[10,3,128]{2,1,0:T(4,128)S(1)}, f32[10,3,128]{2,1,0:T(4,128)S(1)}, u32[]{:S(2)}, u32[]{:S(2)}) collective-permute-start(f32[10,3,128]{2,1,0:T(4,128)S(1)} %get-tuple-element.52), channel_id=1, source_target_pairs={{0,1},{1,2},{2,3},{3,4},{4,5},{5,6},{6,7},{7,0},{8,9},{9,10},{10,1... | collective-permute-start | bytes 46088 | tf_op jit(solution)/shard_map/ppermute | solution.py:35
  51.2 5.9 %collective-permute-start.3 = (f32[10,3,128]{2,1,0:T(4,128)S(1)}, f32[10,3,128]{2,1,0:T(4,128)S(1)}, u32[]{:S(2)}, u32[]{:S(2)}) collective-permute-start(f32[10,3,128]{2,1,0:T(4,128)S(1)} %get-tuple-element.53), channel_id=1, source_target_pairs={{1,0},{2,1},{3,2},{4,3},{5,4},{6,5},{7,6},{0,7},{9,8},{10,9},{11,1... | collective-permute-start | bytes 46088 | tf_op jit(solution)/shard_map/ppermute | solution.py:36
  58.7 8.5 %collective-permute-start.5 = (f32[8,32,256]{2,1,0:T(8,128)S(1)}, f32[8,32,256]{2,1,0:T(8,128)S(1)}, u32[]{:S(2)}, u32[]{:S(2)}) collective-permute-start(f32[8,32,256]{2,1,0:T(8,128)S(1)} %copy.51), channel_id=1, source_target_pairs={{8,0},{16,8},{24,16},{32,24},{40,32},{48,40},{56,48},{64,56},{72,6... | collective-permute-start | bytes 786440 | tf_op jit(solution)/shard_map/ppermute | solution.py:36
  63.3 9.5 %collective-permute-start.4 = (f32[8,32,256]{2,1,0:T(8,128)S(1)}, f32[8,32,256]{2,1,0:T(8,128)S(1)}, u32[]{:S(2)}, u32[]{:S(2)}) collective-permute-start(f32[8,32,256]{2,1,0:T(8,128)S(1)} %copy.51), channel_id=1, source_target_pairs={{0,8},{8,16},{16,24},{24,32},{32,40},{40,48},{48,56},{56,64},{64,7... | collective-permute-start | bytes 786440 | tf_op jit(solution)/shard_map/ppermute | solution.py:35
  72.8 5.7 %collective-permute-start.6 = (f32[24,8,256]{2,1,0:T(8,128)S(1)}, f32[24,8,256]{2,1,0:T(8,128)S(1)}, u32[]{:S(2)}, u32[]{:S(2)}) collective-permute-start(f32[24,8,256]{2,1,0:T(8,128)S(1)} %get-tuple-element.28), channel_id=1, source_target_pairs={{0,1},{1,2},{2,3},{3,4},{4,5},{5,6},{6,7},{7,0},{8,9},{9,10},{10,1... | collective-permute-start | bytes 589832 | tf_op jit(solution)/shard_map/ppermute | solution.py:35
  72.9 8.0 %collective-permute-start.7 = (f32[24,8,256]{2,1,0:T(8,128)S(1)}, f32[24,8,256]{2,1,0:T(8,128)S(1)}, u32[]{:S(2)}, u32[]{:S(2)}) collective-permute-start(f32[24,8,256]{2,1,0:T(8,128)S(1)} %get-tuple-element.29), channel_id=1, source_target_pairs={{1,0},{2,1},{3,2},{4,3},{5,4},{6,5},{7,6},{0,7},{9,8},{10,9},{11,1... | collective-permute-start | bytes 589832 | tf_op jit(solution)/shard_map/ppermute | solution.py:36
where the time goes:
time: 90.1 us; the launch traced here: 90 us
  blocking collectives  39.7 us (44%)
  waiting for transfers between devices  21.2 us (24%)
  starting transfers between devices  14.2 us (16%)
  other arithmetic  11.1 us (12%)
  local copies, waits for them, and re-layouts  3.61 us (4%)
    all_to_all x1, blocking collectives, sent_and_summed(): lax.all_to_all(blocks, axis, split_axis=0, concat_axis=0, tiled=True)  39.7 us
    ppermute x4, starting transfers between devices, padded_2(): after = lax.ppermute(initial, axis, down)  13.7 us
    ppermute x4, waiting for transfers between devices, padded_2(): before = lax.ppermute(last, axis, up)  12.5 us
    ppermute x4, waiting for transfers between devices, padded_2(): after = lax.ppermute(initial, axis, down)  8.69 us
    mul x1, other arithmetic, pointwise(): flux_weight * grad_c  3.71 us
    reduce_sum x1, other arithmetic, on_device(): jnp.sum(weights[:, None, None, None] * jnp.square(orbitals.astype(jnp.flo...  3.41 us
    slice x16, local copies, waits for them, and re-layouts, central(): behind_part = jnp.roll(window_base, offset, 2)  2.56 us
  transfers between devices with their start and end apart: 8, of which 7 were waited for; matrix products, arithmetic and copies ran while one was open for 0% of the time, Pallas kernels for 0%

commit v1 on v0

v1 whole, which is shorter than its diff:
```python
import jax
import jax.numpy as jnp
from jax import lax
from jax.experimental import pallas as pl
from jax.experimental.pallas import tpu as pltpu
from jax.sharding import PartitionSpec as P

MESH = pl.DeviceIdType.MESH
W3, W25, W150 = 3.0 / 256.0, -25.0 / 256.0, 150.0 / 256.0
C1, C2, C3, C4 = 4.0 / 5.0, -1.0 / 5.0, 4.0 / 105.0, -1.0 / 280.0

STEPS = (4, 3, 5, 2, 6, 1, 7, 0)
PARTNERS = tuple((j, e) for j in (1, -1, 2, -2, 0) for e in (1, -1, 0) if (j, e) != (0, 0))


def gather_kernel(occ_ref, orb_ref, dens_ref, orb, part, from_core, from_x, from_z,
                  in_sem, core_s, core_r, x_s, x_r, z_s, z_r, halo_s, halo_r):
    band = lax.axis_index("band")
    dom = lax.axis_index("dom")
    z, h, c = band // 4, (band // 2) % 2, band % 2
    other_c, other_h = 1 - c, 1 - h
    core_peer = z * 4 + h * 2 + other_c
    x_peer = z * 4 + other_h * 2 + c

    def z_peer(k):
        return (band + 4 * k) % 32

    def halo_peer(j, e):
        return (band + j + 32) % 32, (dom + e + 8) % 8

    loads = []
    for s, k in enumerate(STEPS):
        first = ((z + k) % 8) * 16
        load = pltpu.make_async_copy(orb_ref.at[:, pl.ds(first, 16)], orb.at[s], in_sem.at[s])
        load.start()
        loads.append(load)

    barrier = pltpu.get_barrier_semaphore()
    peers = [(core_peer, dom), (x_peer, dom)]
    peers += [(z_peer(k), dom) for k in STEPS if k]
    peers += [halo_peer(j, e) for j, e in PARTNERS]
    for b, d in peers:
        pl.semaphore_signal(barrier, inc=1, device_id={"band": b, "dom": d}, device_id_type=MESH)

    weights = [occ_ref[i] * (1.0 / 256.0) for i in range(8)]

    for s in range(8):
        loads[s].wait()

        def planes(block, _):
            for p in range(4):
                total = jnp.zeros((16, 128), jnp.float32)
                for i in range(8):
                    value = orb[s, i, block * 4 + p].astype(jnp.float32)
                    total = total + weights[i] * (value * value)
                part[s, block % 2, block // 2, p] = total
            return 0

        lax.fori_loop(0, 4, planes, 0)

    pl.semaphore_wait(barrier, len(peers))

    to_core = []
    for s in range(8):
        copy = pltpu.make_async_remote_copy(
            src_ref=part.at[s, other_c], dst_ref=from_core.at[s], send_sem=core_s.at[s],
            recv_sem=core_r.at[s], device_id={"band": core_peer, "dom": dom}, device_id_type=MESH)
        copy.start()
        to_core.append(copy)

    to_x = []
    for s in range(8):
        to_core[s].wait_recv()
        from_core[s] = from_core[s] + part[s, c]
        copy = pltpu.make_async_remote_copy(
            src_ref=from_core.at[s, other_h], dst_ref=from_x.at[s], send_sem=x_s.at[s],
            recv_sem=x_r.at[s], device_id={"band": x_peer, "dom": dom}, device_id_type=MESH)
        copy.start()
        to_x.append(copy)

    to_z = []
    for s, k in enumerate(STEPS):
        to_x[s].wait_recv()
        from_x[s] = from_x[s] + from_core[s, h]
        if k:
            copy = pltpu.make_async_remote_copy(
                src_ref=from_x.at[s], dst_ref=from_z.at[s], send_sem=z_s.at[s],
                recv_sem=z_r.at[s], device_id={"band": z_peer(k), "dom": dom}, device_id_type=MESH)
            copy.start()
            to_z.append(copy)

    total = from_x[7]
    for s in range(7):
        to_z[s].wait_recv()
        total = total + from_z[s]
    dens_ref[6:10, 8:24, :] = total

    halos = []
    for n, (j, e) in enumerate(PARTNERS):
        p0, p1, q0 = {0: (0, 4, 6), 1: (0, 4, 2), -1: (0, 4, 10), 2: (2, 4, 0), -2: (0, 3, 14)}[j]
        r0, r1, t0 = {0: (8, 24, 8), 1: (16, 24, 0), -1: (8, 16, 24)}[e]
        b, d = halo_peer(j, e)
        copy = pltpu.make_async_remote_copy(
            src_ref=dens_ref.at[pl.ds(6 + p0, p1 - p0), pl.ds(r0, r1 - r0)],
            dst_ref=dens_ref.at[pl.ds(q0, p1 - p0), pl.ds(t0, r1 - r0)],
            send_sem=halo_s.at[n], recv_sem=halo_r.at[n],
            device_id={"band": b, "dom": d}, device_id_type=MESH)
        copy.start()
        halos.append(copy)
    for copy in to_core + to_x + to_z:
        copy.wait_send()
    for copy in halos:
        copy.wait()


def gathered(orbitals, occupations):
    f32 = jnp.float32
    dma = pltpu.SemaphoreType.DMA
    return pl.pallas_call(
        gather_kernel,
        out_shape=jax.ShapeDtypeStruct((17, 32, 128), f32),
        in_specs=[pl.BlockSpec(memory_space=pltpu.SMEM), pl.BlockSpec(memory_space=pl.ANY)],
        out_specs=pl.BlockSpec(memory_space=pltpu.VMEM),
        scratch_shapes=[
            pltpu.VMEM((8, 8, 16, 16, 128), jnp.bfloat16),
            pltpu.VMEM((8, 2, 2, 4, 16, 128), f32),
            pltpu.VMEM((8, 2, 4, 16, 128), f32),
            pltpu.VMEM((8, 4, 16, 128), f32),
            pltpu.VMEM((7, 4, 16, 128), f32),
            dma((8,)), dma((8,)), dma((8,)), dma((8,)), dma((8,)), dma((7,)), dma((7,)),
            dma((len(PARTNERS),)), dma((len(PARTNERS),)),
        ],
        compiler_params=pltpu.CompilerParams(collective_id=0, has_side_effects=True,
                                             vmem_limit_bytes=67043328),
    )(occupations, orbitals)


def odd_of(v):
    return W3 * (v[0] + v[5]) + W25 * (v[1] + v[4]) + W150 * (v[2] + v[3])


def weighted(d1, d2, d3, d4):
    return C1 * d1 + C2 * d2 + C3 * d3 + C4 * d4


def turned(v, shift):
    return pltpu.roll(v, shift % 128, 1)


def along_lanes(even, odd):
    ep1, em1, ep2, em2 = turned(even, -1), turned(even, 1), turned(even, -2), turned(even, 2)
    op1, om1, op2, om2 = turned(odd, -1), turned(odd, 1), turned(odd, -2), turned(odd, 2)
    at_even = weighted(odd - om1, ep1 - em1, op1 - om2, ep2 - em2)
    at_odd = weighted(ep1 - even, op1 - om1, ep2 - em1, op2 - om2)
    return at_even, at_odd


def across_planes(ref, p, r0, rows):
    def at(o):
        return ref[p + o, pl.ds(r0, rows), :]
    return weighted(*(at(o) - at(-o) for o in (1, 2, 3, 4)))


def across_rows(ref, p, r0, rows):
    def at(o):
        return ref[p, pl.ds(r0 + o, rows), :]
    return weighted(*(at(o) - at(-o) for o in (1, 2, 3, 4)))


def potential_kernel(dens, out, f1, fe, fo, ae, ao, be, bo, ce, co, le, lo):
    def first(i, _):
        v = [dens[i + o] for o in range(6)]
        f1[2 * i] = v[2]
        f1[2 * i + 1] = odd_of(v)
        return 0
    lax.fori_loop(0, 12, first, 0)

    def second(p, _):
        v = [f1[p, pl.ds(2 + o, 24), :] for o in range(6)]
        fe[p, pl.ds(0, 24, stride=2), :] = v[2]
        fe[p, pl.ds(1, 24, stride=2), :] = odd_of(v)
        return 0
    lax.fori_loop(0, 24, second, 0)

    def third(p, _):
        v = fe[p]
        fo[p] = odd_of([turned(v, 2), turned(v, 1), v, turned(v, -1), turned(v, -2), turned(v, -3)])
        return 0
    lax.fori_loop(0, 24, third, 0)

    def flux(p, r0, rows, inner):
        even, odd = fe[p, pl.ds(r0, rows), :], fo[p, pl.ds(r0, rows), :]
        g3e, g3o = along_lanes(even, odd)
        for f, g3, src, a, b, c, local in ((even, g3e, fe, ae, be, ce, le), (odd, g3o, fo, ao, bo, co, lo)):
            g1 = across_planes(src, p, r0, rows)
            g2 = across_rows(src, p, r0, rows)
            shifted = f * f + 0.01
            sixth = jnp.exp(jnp.log(shifted) * (1.0 / 6.0))
            t2 = sixth * sixth
            t4 = t2 * t2
            scaling = 0.01 * (t4 * t4)
            inverse = 1.0 / (scaling + (0.2195 / 0.804) * (g1 * g1 + g2 * g2 + g3 * g3))
            share = scaling * inverse
            weight = (0.2195 * share) * inverse
            a[p - 4, pl.ds(r0, rows), :] = weight * g1
            if inner:
                b[p - 8, pl.ds(r0, rows), :] = weight * g2
                c[p - 8, pl.ds(r0, rows), :] = weight * g3
                local[p - 8, pl.ds(r0, rows), :] = (-0.75 * sixth) * (1.804 - 0.804 * share)

    def outer_low(p, _):
        flux(p, 8, 32, False)
        return 0

    def inner(p, _):
        flux(p, 4, 40, True)
        return 0
    lax.fori_loop(4, 8, outer_low, 0)
    lax.fori_loop(8, 16, inner, 0)
    lax.fori_loop(16, 20, outer_low, 0)

    half = lax.broadcasted_iota(jnp.int32, (32, 128), 1)
    is_even = half % 2 == 0
    low = half // 2
    high = low + 64

    def last(p, _):
        rows = pl.ds(8, 32)
        d3e, d3o = along_lanes(ce[p, rows, :], co[p, rows, :])
        res = []
        for d3, a, b, local in ((d3e, ae, be, le), (d3o, ao, bo, lo)):
            div = across_planes(a, p + 4, 8, 32) + across_rows(b, p, 8, 32) + d3
            res.append(local[p, rows, :] + 0.2 * div)
        for at, lanes in ((0, low), (128, high)):
            e = jnp.take_along_axis(res[0], lanes, axis=1)
            o = jnp.take_along_axis(res[1], lanes, axis=1)
            out[p, :, pl.ds(at, 128)] = jnp.where(is_even, e, o)
        return 0
    lax.fori_loop(0, 8, last, 0)


def potential_of(dens):
    f32 = jnp.float32
    fine = pltpu.VMEM((24, 48, 128), f32)
    wide = pltpu.VMEM((16, 48, 128), f32)
    narrow = pltpu.VMEM((8, 48, 128), f32)
    return pl.pallas_call(
        potential_kernel,
        out_shape=jax.ShapeDtypeStruct((8, 32, 256), f32),
        in_specs=[pl.BlockSpec(memory_space=pltpu.VMEM)],
        out_specs=pl.BlockSpec(memory_space=pltpu.VMEM),
        scratch_shapes=[pltpu.VMEM((24, 32, 128), f32), fine, fine, wide, wide,
                        narrow, narrow, narrow, narrow, narrow, narrow],
        compiler_params=pltpu.CompilerParams(vmem_limit_bytes=40 * 1024 * 1024),
    )(dens)


def on_device(orbitals, occupations):
    return potential_of(gathered(orbitals, occupations))


def solution(mesh):
    return jax.shard_map(
        on_device,
        mesh=mesh,
        in_specs=(P("band", None, "dom", None), P("band")),
        out_specs=P("band", "dom", None),
        check_vma=False,
    )
```

time: 90.1 us -> 40 us (0.44)
  the two profiles are of different devices: /device:TPU:24 before, /device:TPU:1 now
where the time goes in v1:
time: 40 us; the launch traced here: 39.8 us
  Pallas kernels  38.9 us (97%)
  local copies, waits for them, and re-layouts  0.95 us (2%)
    pallas_call x1, Pallas kernels, gathered(): pl.pallas_call(gather_kernel, out_shape=jax.ShapeDtypeStruct((17, 32, 128...  31.8 us
    pallas_call x1, Pallas kernels, potential_of(): pl.pallas_call(potential_kernel, out_shape=jax.ShapeDtypeStruct((8, 32, 2...  7.09 us
    unnamed x2, local copies, waits for them, and re-layouts  0.95 us

profile of v1, /device:TPU:1, one launch (start us, length us, event | category | flops | bytes accessed | tf_op | source)
XLA Modules:
  0.0 39.8 jit_solution(12704164328606941303)
XLA Ops:
  0.0 31.8 %shard_map.28.dens = f32[17,32,128]{2,1,0:T(8,128)} custom-call(f32[8]{0:T(128)} %occ_ref.1, bf16[8,128,16,128]{3,2,1,0:T(8,128)(2,1)} %orb_ref.1), custom_call_target="tpu_custom_call" | custom-call | tf_op jit(solution)/shard_map/pallas_call | solution.py:119
  31.8 0.0 copy-start
  31.8 0.9 %copy-done = f32[17,32,128]{2,1,0:T(8,128)S(1)} copy-done((f32[17,32,128]{2,1,0:T(8,128)S(1)}, f32[17,32,128]{2,1,0:T(8,128)}, u32[]{:S(2)}) %copy-start) | copy-done | bytes 278552
  32.8 7.1 %shard_map.29 = f32[8,32,256]{2,1,0:T(8,128)} custom-call(f32[17,32,128]{2,1,0:T(8,128)S(1)} %copy-done), custom_call_target="tpu_custom_call" | custom-call | tf_op jit(solution)/shard_map/pallas_call | solution.py:247
Async XLA Ops:
  31.8 1.0 %copy-start = (f32[17,32,128]{2,1,0:T(8,128)S(1)}, f32[17,32,128]{2,1,0:T(8,128)}, u32[]{:S(2)}) copy-start(f32[17,32,128]{2,1,0:T(8,128)} %shard_map.28.dens) | copy-start | bytes 835588

commit v2 on v1

v2 whole, which is shorter than its diff:
```python
import jax
import jax.numpy as jnp
from jax import lax
from jax.experimental import pallas as pl
from jax.experimental.pallas import tpu as pltpu
from jax.sharding import PartitionSpec as P

MESH = pl.DeviceIdType.MESH
F32, BF16 = jnp.float32, jnp.bfloat16
W3, W25, W150 = 3.0 / 256.0, -25.0 / 256.0, 150.0 / 256.0
REFINE = {-2: W3, -1: W25, 0: W150, 1: W150, 2: W25, 3: W3}
D1, D2, D3, D4 = 224.0, -56.0, 32.0 / 3.0, -1.0
DERIV = {1: D1, 2: D2, 3: D3, 4: D4}

STEPS = (4, 3, 5, 2, 6, 1, 7, 0)
PARTNERS = tuple((j, e) for j in (1, -1, 2, -2, 0) for e in (1, -1, 0) if (j, e) != (0, 0))


def fine_cell(r):
    if r % 2 == 0:
        return {r // 2: 1.0}
    return {(r - 1) // 2 + o: w for o, w in REFINE.items()}


def composed(r):
    out = {}
    for o, c in DERIV.items():
        for sign in (1, -1):
            for m, w in fine_cell(r + sign * o).items():
                out[m] = out.get(m, 0.0) + sign * c * w
    return out


def circulant(factors):
    source = lax.broadcasted_iota(jnp.int32, (128, 128), 0)
    target = lax.broadcasted_iota(jnp.int32, (128, 128), 1)
    offset = (source - target + 128) % 128
    out = jnp.zeros((128, 128), F32)
    for m, w in factors.items():
        out = jnp.where(offset == m % 128, w, out)
    return out


def two_terms(v):
    high = v.astype(BF16)
    return high, (v - high.astype(F32)).astype(BF16)


def build_matrices(wide_w, low_w, deriv_w, weave_w):
    refine = circulant(REFINE).astype(BF16)
    wide_w[0:128, 0:128] = refine
    wide_w[128:256, 0:128] = refine
    for r in (0, 1):
        high, low = two_terms(circulant(composed(r)))
        columns = slice(128 + 128 * r, 256 + 128 * r)
        wide_w[0:128, columns] = high
        wide_w[128:256, columns] = high
        low_w[:, 128 * r:128 * r + 128] = low
    for r in (0, 1):
        source = 2 * lax.broadcasted_iota(jnp.int32, (128, 256), 0) + r
        target = lax.broadcasted_iota(jnp.int32, (128, 256), 1)
        offset = (source - target + 256) % 256
        out = jnp.zeros((128, 256), F32)
        for o, c in ((1, 672.0), (2, -168.0), (3, 32.0), (4, -3.0)):
            out = jnp.where(offset == o, c, jnp.where(offset == 256 - o, -c, out))
        deriv_w[128 * r:128 * r + 128, :] = out.astype(BF16)
        weave_w[128 * r:128 * r + 128, :] = jnp.where(offset == 0, 1.0, 0.0).astype(BF16)


def kernel(occ_hbm, orb_ref, out_ref, occ_ref, occ_sem, dens_ref, orb, part, from_core, from_x, from_z,
           in_sem, core_s, core_r, x_s, x_r, z_s, z_r, halo_s, halo_r, matrices, fields):
    band = lax.axis_index("band")
    dom = lax.axis_index("dom")
    z, h, c = band // 4, (band // 2) % 2, band % 2
    other_c, other_h = 1 - c, 1 - h
    core_peer = z * 4 + h * 2 + other_c
    x_peer = z * 4 + other_h * 2 + c

    def z_peer(k):
        return (band + 4 * k) % 32

    def halo_peer(j, e):
        return (band + j + 32) % 32, (dom + e + 8) % 8

    def remote(src, dst, send_sem, recv_sem, b, d):
        copy = pltpu.make_async_remote_copy(
            src_ref=src, dst_ref=dst, send_sem=send_sem, recv_sem=recv_sem,
            device_id={"band": b, "dom": d}, device_id_type=MESH)
        copy.start()
        return copy

    occ_load = pltpu.make_async_copy(occ_hbm, occ_ref, occ_sem)
    occ_load.start()
    loads = []
    for s, k in enumerate(STEPS):
        first = ((z + k) % 8) * 16
        load = pltpu.make_async_copy(orb_ref.at[:, pl.ds(first, 16)], orb.at[s], in_sem.at[s])
        load.start()
        loads.append(load)

    barrier = pltpu.get_barrier_semaphore()
    peers = [(core_peer, dom), (x_peer, dom)]
    peers += [(z_peer(k), dom) for k in STEPS if k]
    peers += [halo_peer(j, e) for j, e in PARTNERS]
    for b, d in peers:
        pl.semaphore_signal(barrier, inc=1, device_id={"band": b, "dom": d}, device_id_type=MESH)

    occ_load.wait()
    weights = [occ_ref[i] * (1.0 / 256.0) for i in range(8)]

    def band_sum(s):
        loads[s].wait()

        def planes(block, _):
            for p in range(4):
                total = jnp.zeros((16, 128), F32)
                for i in range(8):
                    value = orb[s, i, block * 4 + p].astype(F32)
                    total = total + weights[i] * (value * value)
                part[s, block % 2, block // 2, p] = total
            return 0

        lax.fori_loop(0, 4, planes, 0)

    to_core, to_x, to_z = [], [], []

    def send_core(s):
        to_core.append(remote(part.at[s, other_c], from_core.at[s], core_s.at[s], core_r.at[s],
                              core_peer, dom))

    def send_x(s):
        to_core[s].wait_recv()
        from_core[s] = from_core[s] + part[s, c]
        to_x.append(remote(from_core.at[s, other_h], from_x.at[s], x_s.at[s], x_r.at[s], x_peer, dom))

    for s in range(6):
        band_sum(s)
    pl.semaphore_wait(barrier, len(peers))
    for s in range(6):
        send_core(s)
    band_sum(6)
    send_core(6)
    send_x(0)
    send_x(1)
    band_sum(7)
    send_core(7)
    for s in range(2, 8):
        send_x(s)
    build_matrices(*matrices)
    for s, k in enumerate(STEPS):
        to_x[s].wait_recv()
        from_x[s] = from_x[s] + from_core[s, h]
        if k:
            to_z.append(remote(from_x.at[s], from_z.at[s], z_s.at[s], z_r.at[s], z_peer(k), dom))

    total = from_x[7]
    for s in range(7):
        to_z[s].wait_recv()
        total = total + from_z[s]
    dens_ref[6:10, 8:24, :] = total

    halos = []
    for n, (j, e) in enumerate(PARTNERS):
        p0, p1, q0 = {0: (0, 4, 6), 1: (0, 4, 2), -1: (0, 4, 10), 2: (2, 4, 0), -2: (0, 3, 14)}[j]
        r0, r1, t0 = {0: (8, 24, 8), 1: (16, 24, 0), -1: (8, 16, 24)}[e]
        b, d = halo_peer(j, e)
        halos.append(remote(dens_ref.at[pl.ds(6 + p0, p1 - p0), pl.ds(r0, r1 - r0)],
                            dens_ref.at[pl.ds(q0, p1 - p0), pl.ds(t0, r1 - r0)],
                            halo_s.at[n], halo_r.at[n], b, d))
    for copy in to_core + to_x + to_z:
        copy.wait_send()
    for copy in halos:
        copy.wait()
    potential_from(dens_ref, out_ref, matrices, *fields)


def odd_of(v):
    return W3 * (v[0] + v[5]) + W25 * (v[1] + v[4]) + W150 * (v[2] + v[3])


def scaled_derivative(at):
    d = [at(o) - at(-o) for o in (1, 2, 3, 4)]
    return (D1 * d[0] + D2 * d[1]) + (D3 * d[2] - d[3])


def across_planes(ref, p, r0, rows):
    return scaled_derivative(lambda o: ref[p + o, pl.ds(r0, rows), :])


def across_rows(ref, p, r0, rows):
    return scaled_derivative(lambda o: ref[p, pl.ds(r0 + o, rows), :])


def dot(a, b):
    return jnp.dot(a, b, preferred_element_type=F32)


def potential_from(dens, out, matrices, f1, fe, fo, g3, ae, ao, be, bo, ce, co, le, lo):
    wide_w, low_w, deriv_w, weave_w = matrices

    def first(i, _):
        v = [dens[i + o] for o in range(6)]
        f1[2 * i] = v[2]
        f1[2 * i + 1] = odd_of(v)
        return 0
    lax.fori_loop(0, 12, first, 0)

    def second(p, _):
        v = [f1[p, pl.ds(2 + o, 24), :] for o in range(6)]
        fe[p, pl.ds(0, 24, stride=2), :] = v[2]
        fe[p, pl.ds(1, 24, stride=2), :] = odd_of(v)
        return 0
    lax.fori_loop(0, 24, second, 0)

    def split(p):
        high, low = two_terms(fe[pl.ds(p, 4)].reshape(192, 128))
        return high, jnp.concatenate([high, low], axis=1)

    def third_outer(p):
        _, both = split(p)
        fo[pl.ds(p, 4)] = dot(both, wide_w[:, 0:128]).reshape(4, 48, 128)

    def third_inner(i, _):
        p = 4 + 4 * i
        high, both = split(p)
        fo[pl.ds(p, 4)] = dot(both, wide_w[:, 0:128]).reshape(4, 48, 128)
        g = dot(both, wide_w[:, 128:384]) + dot(high, low_w[...])
        g3[0, pl.ds(4 * i, 4)] = g[:, 0:128].reshape(4, 48, 128)
        g3[1, pl.ds(4 * i, 4)] = g[:, 128:256].reshape(4, 48, 128)
        return 0
    third_outer(0)
    third_outer(20)
    lax.fori_loop(0, 4, third_inner, 0)

    def flux(p, r0, rows, inner):
        rs = pl.ds(r0, rows)
        for n, (src, a, b, c, local) in enumerate(((fe, ae, be, ce, le), (fo, ao, bo, co, lo))):
            f = src[p, rs, :]
            g1 = across_planes(src, p, r0, rows)
            g2 = across_rows(src, p, r0, rows)
            g_3 = g3[n, p - 4, rs, :]
            shifted = f * f + 0.01
            sixth = jnp.exp(jnp.log(shifted) * (1.0 / 6.0))
            t2 = sixth * sixth
            t4 = t2 * t2
            scaling = 0.01 * (t4 * t4)
            inverse = 1.0 / (scaling + (0.2195 / 0.804 / 78400.0) * (g1 * g1 + g2 * g2 + g_3 * g_3))
            share = scaling * inverse
            weight = ((0.2195 / 280.0) * share) * inverse
            a[p - 4, rs, :] = weight * g1
            if inner:
                b[p - 8, rs, :] = weight * g2
                c[p - 8, rs, :] = weight * g_3
                local[p - 8, rs, :] = sixth * (0.603 * share - 1.353)

    def outer(p, _):
        flux(p, 8, 32, False)
        return 0

    def inner(p, _):
        flux(p, 4, 40, True)
        return 0
    lax.fori_loop(4, 8, outer, 0)
    lax.fori_loop(8, 16, inner, 0)
    lax.fori_loop(16, 20, outer, 0)

    def last(i, _):
        p = 4 * i
        rows = pl.ds(8, 32)
        kept = ([], [], [], [])
        for n, (a, b, c, local) in enumerate(((ae, be, ce, le), (ao, bo, co, lo))):
            here = []
            for q in range(4):
                div = across_planes(a, p + q + 4, 8, 32) + across_rows(b, p + q, 8, 32)
                here.append(local[p + q, rows, :] + (0.2 / 280.0) * div)
            kept[0].append(jnp.concatenate(here, axis=0))
            kept[1].append(c[pl.ds(p, 4), rows, :].reshape(128, 128))
        res = []
        for values, w in ((kept[0], weave_w), (kept[1], deriv_w)):
            e, o = two_terms(values[0]), two_terms(values[1])
            res.append(dot(jnp.concatenate([e[0], o[0]], axis=1), w[...])
                       + dot(jnp.concatenate([e[1], o[1]], axis=1), w[...]))
        out[pl.ds(p, 4)] = (res[0] + (0.2 / 840.0) * res[1]).reshape(4, 32, 256)
        return 0
    lax.fori_loop(0, 2, last, 0)


def on_device(orbitals, occupations):
    dma = pltpu.SemaphoreType.DMA
    fine = pltpu.VMEM((24, 48, 128), F32)
    wide = pltpu.VMEM((16, 48, 128), F32)
    narrow = pltpu.VMEM((8, 48, 128), F32)
    return pl.pallas_call(
        kernel,
        out_shape=jax.ShapeDtypeStruct((8, 32, 256), F32),
        in_specs=[pl.BlockSpec(memory_space=pltpu.HBM), pl.BlockSpec(memory_space=pltpu.HBM)],
        out_specs=pl.BlockSpec(memory_space=pltpu.VMEM),
        scratch_shapes=[
            pltpu.SMEM((8,), F32), dma(()),
            pltpu.VMEM((17, 32, 128), F32),
            pltpu.VMEM((8, 8, 16, 16, 128), BF16),
            pltpu.VMEM((8, 2, 2, 4, 16, 128), F32),
            pltpu.VMEM((8, 2, 4, 16, 128), F32),
            pltpu.VMEM((8, 4, 16, 128), F32),
            pltpu.VMEM((7, 4, 16, 128), F32),
            dma((8,)), dma((8,)), dma((8,)), dma((8,)), dma((8,)), dma((7,)), dma((7,)),
            dma((len(PARTNERS),)), dma((len(PARTNERS),)),
            (pltpu.VMEM((256, 384), BF16), pltpu.VMEM((128, 256), BF16),
             pltpu.VMEM((256, 256), BF16), pltpu.VMEM((256, 256), BF16)),
            (pltpu.VMEM((24, 32, 128), F32), fine, fine, pltpu.VMEM((2, 16, 48, 128), F32), wide, wide,
             narrow, narrow, narrow, narrow, narrow, narrow),
        ],
        compiler_params=pltpu.CompilerParams(collective_id=0, has_side_effects=True,
                                             vmem_limit_bytes=53 * 1024 * 1024),
    )(pltpu.with_memory_space_constraint(occupations, pltpu.HBM), pltpu.with_memory_space_constraint(orbitals, pltpu.HBM))


def solution(mesh):
    return jax.shard_map(
        on_device,
        mesh=mesh,
        in_specs=(P("band", None, "dom", None), P("band")),
        out_specs=P("band", "dom", None),
        check_vma=False,
    )
```

time: 40 us -> 34.5 us (0.86)
  Pallas kernels: 38.9 us -> 33.7 us
    pallas_call x2 -> x1, Pallas kernels: 38.9 us -> 33.7 us  [on_device(): pl.pallas_call(kernel, out_shape=jax.ShapeDtypeStruct((8, 32, 256), F32),...]
    unnamed x2 -> x1, local copies, waits for them, and re-layouts: 0.95 us -> 0.71 us
where the time goes in v2:
time: 34.5 us; the launch traced here: 34.4 us
  Pallas kernels  33.7 us (98%)
  local copies, waits for them, and re-layouts  0.71 us (2%)
    pallas_call x1, Pallas kernels, on_device(): pl.pallas_call(kernel, out_shape=jax.ShapeDtypeStruct((8, 32, 256), F32),...  33.7 us
    unnamed x1, local copies, waits for them, and re-layouts  0.71 us

profile of v2, /device:TPU:1, one launch (start us, length us, event | category | flops | bytes accessed | tf_op | source)
XLA Modules:
  0.0 34.4 jit_solution(1126941526047987872)
XLA Ops:
  0.0 33.7 %shard_map.28 = f32[8,32,256]{2,1,0:T(8,128)S(1)} custom-call(f32[8]{0:T(128)} %occ_hbm.1, bf16[8,128,16,128]{3,2,1,0:T(8,128)(2,1)} %orb_ref.1), custom_call_target="tpu_custom_call" | custom-call | tf_op jit(solution)/shard_map/pallas_call | solution.py:293
  33.7 0.7 %copy.4 = f32[8,32,256]{2,1,0:T(8,128)} copy(f32[8,32,256]{2,1,0:T(8,128)S(1)} %shard_map.28) | data formatting | bytes 524288

commit v3 on v2

--- a/solution.py
+++ b/solution.py
@@ -12,7 +12,10 @@
 D1, D2, D3, D4 = 224.0, -56.0, 32.0 / 3.0, -1.0
 DERIV = {1: D1, 2: D2, 3: D3, 4: D4}
 
-STEPS = (4, 3, 5, 2, 6, 1, 7, 0)
+STEPS = (4, 3, 5, 1, 7, 2, 6, 0)
+FAR = (4, 3, 5, 2, 6)
+NEAR = (1, 7)
+AROUND = tuple((j, e) for j in (1, -1, 0) for e in (1, -1, 0) if (j, e) != (0, 0))
 PARTNERS = tuple((j, e) for j in (1, -1, 2, -2, 0) for e in (1, -1, 0) if (j, e) != (0, 0))
 
 
@@ -67,8 +70,8 @@
         weave_w[128 * r:128 * r + 128, :] = jnp.where(offset == 0, 1.0, 0.0).astype(BF16)
 
 
-def kernel(occ_hbm, orb_ref, out_ref, occ_ref, occ_sem, dens_ref, orb, part, from_core, from_x, from_z,
-           in_sem, core_s, core_r, x_s, x_r, z_s, z_r, halo_s, halo_r, matrices, fields):
+def kernel(occ_hbm, orb_ref, out_ref, occ_ref, occ_sem, dens_ref, orb, part, from_core, from_x, from_z, from_near,
+           in_sem, core_s, core_r, x_s, x_r, z_s, z_r, near_s, near_r, near_ok, far_ok, halo_s, halo_r, matrices, fields):
     band = lax.axis_index("band")
     dom = lax.axis_index("dom")
     z, h, c = band // 4, (band // 2) % 2, band % 2
@@ -99,11 +102,21 @@
         loads.append(load)
 
     barrier = pltpu.get_barrier_semaphore()
-    peers = [(core_peer, dom), (x_peer, dom)]
-    peers += [(z_peer(k), dom) for k in STEPS if k]
-    peers += [halo_peer(j, e) for j, e in PARTNERS]
-    for b, d in peers:
+
+    def greet(b, d):
         pl.semaphore_signal(barrier, inc=1, device_id={"band": b, "dom": d}, device_id_type=MESH)
+
+    greet(z * 4 + other_h * 2, dom)
+
+    @pl.when(c == 1)
+    def _():
+        greet(z * 4 + h * 2, dom)
+
+    for k in STEPS:
+        if k:
+            greet(z_peer(k) - c + 1, dom)
+    for j, e in AROUND:
+        greet((band - c + 1 + 2 * j + 32) % 32, (dom + e + 8) % 8)
 
     occ_load.wait()
     weights = [occ_ref[i] * (1.0 / 256.0) for i in range(8)]
@@ -122,7 +135,7 @@
 
         lax.fori_loop(0, 4, planes, 0)
 
-    to_core, to_x, to_z = [], [], []
+    to_core, to_x, to_z, to_near = [], {}, [], []
 
     def send_core(s):
         to_core.append(remote(part.at[s, other_c], from_core.at[s], core_s.at[s], core_r.at[s],
@@ -131,32 +144,52 @@
     def send_x(s):
         to_core[s].wait_recv()
         from_core[s] = from_core[s] + part[s, c]
-        to_x.append(remote(from_core.at[s, other_h], from_x.at[s], x_s.at[s], x_r.at[s], x_peer, dom))
-
-    for s in range(6):
+        if STEPS[s] in FAR:
+            reduce_x(s)
+
+    def reduce_x(s):
+        to_x[s] = remote(from_core.at[s, other_h], from_x.at[s], x_s.at[s], x_r.at[s], x_peer, dom)
+
+    def meet(sem, first_c, count):
+        @pl.when(c == first_c)
+        def _():
+            pl.semaphore_wait(barrier, count)
+            pl.semaphore_signal(sem, inc=1, device_id={"band": core_peer, "dom": dom}, device_id_type=MESH)
+
+        @pl.when(c != first_c)
+        def _():
+            pl.semaphore_wait(sem, 1)
+
+    for s in range(8):
         band_sum(s)
-    pl.semaphore_wait(barrier, len(peers))
-    for s in range(6):
+        if s == 0:
+            meet(near_ok, 0, 3)
         send_core(s)
-    band_sum(6)
-    send_core(6)
-    send_x(0)
-    send_x(1)
-    band_sum(7)
-    send_core(7)
-    for s in range(2, 8):
-        send_x(s)
+        if s >= 2:
+            send_x(s - 2)
+    send_x(6)
+    send_x(7)
+    meet(far_ok, 1, 2 * 7 + 2 * len(AROUND))
+    for n, k in enumerate(NEAR):
+        to_near.append(remote(from_core.at[STEPS.index(k)], from_near.at[n], near_s.at[n], near_r.at[n],
+                              z_peer(k), dom))
     build_matrices(*matrices)
-    for s, k in enumerate(STEPS):
+    for n, k in enumerate(FAR):
+        if n == 2:
+            for copy in to_near:
+                copy.wait_recv()
+            from_core[7] = from_core[7] + (from_near[0] + from_near[1])
+            reduce_x(7)
+        s = STEPS.index(k)
         to_x[s].wait_recv()
         from_x[s] = from_x[s] + from_core[s, h]
-        if k:
-            to_z.append(remote(from_x.at[s], from_z.at[s], z_s.at[s], z_r.at[s], z_peer(k), dom))
-
-    total = from_x[7]
-    for s in range(7):
-        to_z[s].wait_recv()
-        total = total + from_z[s]
+        to_z.append(remote(from_x.at[s], from_z.at[n], z_s.at[n], z_r.at[n], z_peer(k), dom))
+
+    to_x[7].wait_recv()
+    total = from_x[7] + from_core[7, h]
+    for n in range(len(FAR)):
+        to_z[n].wait_recv()
+        total = total + from_z[n]
     dens_ref[6:10, 8:24, :] = total
 
     halos = []
@@ -167,7 +200,7 @@
         halos.append(remote(dens_ref.at[pl.ds(6 + p0, p1 - p0), pl.ds(r0, r1 - r0)],
                             dens_ref.at[pl.ds(q0, p1 - p0), pl.ds(t0, r1 - r0)],
                             halo_s.at[n], halo_r.at[n], b, d))
-    for copy in to_core + to_x + to_z:
+    for copy in to_core + list(to_x.values()) + to_z + to_near:
         copy.wait_send()
     for copy in halos:
         copy.wait()
@@ -302,8 +335,10 @@
             pltpu.VMEM((8, 2, 2, 4, 16, 128), F32),
             pltpu.VMEM((8, 2, 4, 16, 128), F32),
             pltpu.VMEM((8, 4, 16, 128), F32),
-            pltpu.VMEM((7, 4, 16, 128), F32),
-            dma((8,)), dma((8,)), dma((8,)), dma((8,)), dma((8,)), dma((7,)), dma((7,)),
+            pltpu.VMEM((5, 4, 16, 128), F32),
+            pltpu.VMEM((2, 2, 4, 16, 128), F32),
+            dma((8,)), dma((8,)), dma((8,)), dma((8,)), dma((8,)), dma((5,)), dma((5,)),
+            dma((2,)), dma((2,)), pltpu.SemaphoreType.REGULAR, pltpu.SemaphoreType.REGULAR,
             dma((len(PARTNERS),)), dma((len(PARTNERS),)),
             (pltpu.VMEM((256, 384), BF16), pltpu.VMEM((128, 256), BF16),
              pltpu.VMEM((256, 256), BF16), pltpu.VMEM((256, 256), BF16)),

time: 34.5 us -> 32.2 us (0.933)
  Pallas kernels: 33.7 us -> 31.4 us
    pallas_call x1, Pallas kernels: 33.7 us -> 31.4 us  [on_device(): pl.pallas_call(kernel, out_shape=jax.ShapeDtypeStruct((8, 32, 256), F32),...]
where the time goes in v3:
time: 32.2 us; the launch traced here: 32.1 us
  Pallas kernels  31.4 us (98%)
  local copies, waits for them, and re-layouts  0.71 us (2%)
    pallas_call x1, Pallas kernels, on_device(): pl.pallas_call(kernel, out_shape=jax.ShapeDtypeStruct((8, 32, 256), F32),...  31.4 us
    unnamed x1, local copies, waits for them, and re-layouts  0.71 us

profile of v3, /device:TPU:1, one launch (start us, length us, event | category | flops | bytes accessed | tf_op | source)
XLA Modules:
  0.0 32.1 jit_solution(4736164089394745365)
XLA Ops:
  0.0 31.4 %shard_map.28 = f32[8,32,256]{2,1,0:T(8,128)S(1)} custom-call(f32[8]{0:T(128)} %occ_hbm.1, bf16[8,128,16,128]{3,2,1,0:T(8,128)(2,1)} %orb_ref.1), custom_call_target="tpu_custom_call" | custom-call | tf_op jit(solution)/shard_map/pallas_call | solution.py:326
  31.4 0.7 %copy.4 = f32[8,32,256]{2,1,0:T(8,128)} copy(f32[8,32,256]{2,1,0:T(8,128)S(1)} %shard_map.28) | data formatting | bytes 524288

commit v4 on v3

--- a/solution.py
+++ b/solution.py
@@ -1,3 +1,5 @@
+import math
+
 import jax
 import jax.numpy as jnp
 from jax import lax
@@ -15,6 +17,7 @@
 STEPS = (4, 3, 5, 1, 7, 2, 6, 0)
 FAR = (4, 3, 5, 2, 6)
 NEAR = (1, 7)
+LAG = 4
 AROUND = tuple((j, e) for j in (1, -1, 0) for e in (1, -1, 0) if (j, e) != (0, 0))
 PARTNERS = tuple((j, e) for j in (1, -1, 2, -2, 0) for e in (1, -1, 0) if (j, e) != (0, 0))
 
@@ -165,10 +168,10 @@
         if s == 0:
             meet(near_ok, 0, 3)
         send_core(s)
-        if s >= 2:
-            send_x(s - 2)
-    send_x(6)
-    send_x(7)
+        if s >= LAG:
+            send_x(s - LAG)
+    for s in range(8 - LAG, 8):
+        send_x(s)
     meet(far_ok, 1, 2 * 7 + 2 * len(AROUND))
     for n, k in enumerate(NEAR):
         to_near.append(remote(from_core.at[STEPS.index(k)], from_near.at[n], near_s.at[n], near_r.at[n],
@@ -195,16 +198,24 @@
     halos = []
     for n, (j, e) in enumerate(PARTNERS):
         p0, p1, q0 = {0: (0, 4, 6), 1: (0, 4, 2), -1: (0, 4, 10), 2: (2, 4, 0), -2: (0, 3, 14)}[j]
-        r0, r1, t0 = {0: (8, 24, 8), 1: (16, 24, 0), -1: (8, 16, 24)}[e]
+        r0, r1, t0 = {0: (8, 24, 8), 1: (18, 24, 2), -1: (8, 15, 24)}[e]
         b, d = halo_peer(j, e)
         halos.append(remote(dens_ref.at[pl.ds(6 + p0, p1 - p0), pl.ds(r0, r1 - r0)],
                             dens_ref.at[pl.ds(q0, p1 - p0), pl.ds(t0, r1 - r0)],
                             halo_s.at[n], halo_r.at[n], b, d))
-    for copy in to_core + list(to_x.values()) + to_z + to_near:
+    def own_rows_here():
+        for copy, (_, e) in zip(halos, PARTNERS):
+            if e == 0:
+                copy.wait_recv()
+
+    def all_here():
+        for copy, (_, e) in zip(halos, PARTNERS):
+            if e != 0:
+                copy.wait_recv()
+
+    potential_from(own_rows_here, all_here, dens_ref, out_ref, matrices, *fields)
+    for copy in to_core + list(to_x.values()) + to_z + to_near + halos:
         copy.wait_send()
-    for copy in halos:
-        copy.wait()
-    potential_from(dens_ref, out_ref, matrices, *fields)
 
 
 def odd_of(v):
@@ -228,44 +239,46 @@
     return jnp.dot(a, b, preferred_element_type=F32)
 
 
-def potential_from(dens, out, matrices, f1, fe, fo, g3, ae, ao, be, bo, ce, co, le, lo):
+def potential_from(own_rows_here, all_here, dens, out, matrices, f1, fe, fo, g3, ae, ao, be, bo, ce, co, le, lo, rest, turn):
     wide_w, low_w, deriv_w, weave_w = matrices
 
-    def first(i, _):
-        v = [dens[i + o] for o in range(6)]
-        f1[2 * i] = v[2]
-        f1[2 * i + 1] = odd_of(v)
-        return 0
-    lax.fori_loop(0, 12, first, 0)
-
-    def second(p, _):
-        v = [f1[p, pl.ds(2 + o, 24), :] for o in range(6)]
-        fe[p, pl.ds(0, 24, stride=2), :] = v[2]
-        fe[p, pl.ds(1, 24, stride=2), :] = odd_of(v)
-        return 0
-    lax.fori_loop(0, 24, second, 0)
-
-    def split(p):
-        high, low = two_terms(fe[pl.ds(p, 4)].reshape(192, 128))
-        return high, jnp.concatenate([high, low], axis=1)
-
-    def third_outer(p):
-        _, both = split(p)
-        fo[pl.ds(p, 4)] = dot(both, wide_w[:, 0:128]).reshape(4, 48, 128)
-
-    def third_inner(i, _):
-        p = 4 + 4 * i
-        high, both = split(p)
-        fo[pl.ds(p, 4)] = dot(both, wide_w[:, 0:128]).reshape(4, 48, 128)
-        g = dot(both, wide_w[:, 128:384]) + dot(high, low_w[...])
-        g3[0, pl.ds(4 * i, 4)] = g[:, 0:128].reshape(4, 48, 128)
-        g3[1, pl.ds(4 * i, 4)] = g[:, 128:256].reshape(4, 48, 128)
-        return 0
-    third_outer(0)
-    third_outer(20)
-    lax.fori_loop(0, 4, third_inner, 0)
-
-    def flux(p, r0, rows, inner):
+    def first(*groups):
+        def body(i, _):
+            for r0, rows in groups:
+                rs = pl.ds(r0, rows)
+                v = [dens[i + o, rs, :] for o in range(6)]
+                f1[2 * i, rs, :] = v[2]
+                f1[2 * i + 1, rs, :] = odd_of(v)
+            return 0
+        lax.fori_loop(0, 12, body, 0)
+
+    def second(*starts):
+        def body(i, _):
+            for p in (2 * i, 2 * i + 1):
+                for r0 in starts:
+                    v = [f1[p, pl.ds(r0 // 2 + 2 + o, 8), :] for o in range(6)]
+                    fe[p, pl.ds(r0, 8, stride=2), :] = v[2]
+                    fe[p, pl.ds(r0 + 1, 8, stride=2), :] = odd_of(v)
+            return 0
+        lax.fori_loop(0, 12, body, 0)
+
+    def third(*starts):
+        cells = jnp.concatenate([fe[:, pl.ds(r0, 16), :].reshape(384, 128) for r0 in starts], axis=0)
+        high, low = two_terms(cells)
+        both = jnp.concatenate([high, low], axis=1)
+        odd = dot(both, wide_w[:, 0:128])
+
+        def inner(v):
+            return jnp.concatenate([v[384 * i + 64:384 * i + 320] for i in range(len(starts))], axis=0)
+
+        g = dot(inner(both), wide_w[:, 128:384]) + dot(inner(high), low_w[...])
+        for i, r0 in enumerate(starts):
+            rs = pl.ds(r0, 16)
+            fo[:, rs, :] = odd[384 * i:384 * i + 384].reshape(24, 16, 128)
+            for r in (0, 1):
+                g3[r, :, rs, :] = g[256 * i:256 * i + 256, 128 * r:128 * r + 128].reshape(16, 16, 128)
+
+    def flux_of(p, r0, rows, inner):
         rs = pl.ds(r0, rows)
         for n, (src, a, b, c, local) in enumerate(((fe, ae, be, ce, le), (fo, ao, bo, co, lo))):
             f = src[p, rs, :]
@@ -273,7 +286,7 @@
             g2 = across_rows(src, p, r0, rows)
             g_3 = g3[n, p - 4, rs, :]
             shifted = f * f + 0.01
-            sixth = jnp.exp(jnp.log(shifted) * (1.0 / 6.0))
+            sixth = jnp.exp2(jnp.log(shifted) * (1.0 / (6.0 * math.log(2.0))))
             t2 = sixth * sixth
             t4 = t2 * t2
             scaling = 0.01 * (t4 * t4)
@@ -286,36 +299,39 @@
                 c[p - 8, rs, :] = weight * g_3
                 local[p - 8, rs, :] = sixth * (0.603 * share - 1.353)
 
-    def outer(p, _):
-        flux(p, 8, 32, False)
+    def flux(step, *groups):
+        for lo_p, hi_p, inner in ((4, 8, False), (8, 16, True), (16, 20, False)):
+            def body(i, _):
+                for q in range(step):
+                    for r0, rows in groups:
+                        flux_of(lo_p + i * step + q, r0, rows, inner)
+                return 0
+            lax.fori_loop(0, (hi_p - lo_p) // step, body, 0)
+
+    own_rows_here()
+    first((8, 16))
+    second(16)
+    third(16)
+    flux(2, (20, 8))
+    all_here()
+    first((0, 8), (24, 8))
+    second(0, 32)
+    third(0, 32)
+    flux(2, (4, 16), (28, 16))
+
+    def last(p, _):
+        rows = pl.ds(8, 32)
+        for n, (a, b, c, local) in enumerate(((ae, be, ce, le), (ao, bo, co, lo))):
+            lanes = slice(128 * n, 128 * n + 128)
+            div = across_planes(a, p + 4, 8, 32) + across_rows(b, p, 8, 32)
+            for ref, value in ((rest, local[p, rows, :] + (0.2 / 280.0) * div), (turn, c[p, rows, :])):
+                high, low = two_terms(value)
+                ref[pl.ds(pl.multiple_of(32 * p, 32), 32), lanes] = high
+                ref[pl.ds(pl.multiple_of(32 * p + 256, 32), 32), lanes] = low
         return 0
-
-    def inner(p, _):
-        flux(p, 4, 40, True)
-        return 0
-    lax.fori_loop(4, 8, outer, 0)
-    lax.fori_loop(8, 16, inner, 0)
-    lax.fori_loop(16, 20, outer, 0)
-
-    def last(i, _):
-        p = 4 * i
-        rows = pl.ds(8, 32)
-        kept = ([], [], [], [])
-        for n, (a, b, c, local) in enumerate(((ae, be, ce, le), (ao, bo, co, lo))):
-            here = []
-            for q in range(4):
-                div = across_planes(a, p + q + 4, 8, 32) + across_rows(b, p + q, 8, 32)
-                here.append(local[p + q, rows, :] + (0.2 / 280.0) * div)
-            kept[0].append(jnp.concatenate(here, axis=0))
-            kept[1].append(c[pl.ds(p, 4), rows, :].reshape(128, 128))
-        res = []
-        for values, w in ((kept[0], weave_w), (kept[1], deriv_w)):
-            e, o = two_terms(values[0]), two_terms(values[1])
-            res.append(dot(jnp.concatenate([e[0], o[0]], axis=1), w[...])
-                       + dot(jnp.concatenate([e[1], o[1]], axis=1), w[...]))
-        out[pl.ds(p, 4)] = (res[0] + (0.2 / 840.0) * res[1]).reshape(4, 32, 256)
-        return 0
-    lax.fori_loop(0, 2, last, 0)
+    lax.fori_loop(0, 8, last, 0)
+    woven, derived = dot(rest[...], weave_w[...]), dot(turn[...], deriv_w[...])
+    out[...] = ((woven[:256] + woven[256:]) + (0.2 / 840.0) * (derived[:256] + derived[256:])).reshape(8, 32, 256)
 
 
 def on_device(orbitals, occupations):
@@ -343,7 +359,7 @@
             (pltpu.VMEM((256, 384), BF16), pltpu.VMEM((128, 256), BF16),
              pltpu.VMEM((256, 256), BF16), pltpu.VMEM((256, 256), BF16)),
             (pltpu.VMEM((24, 32, 128), F32), fine, fine, pltpu.VMEM((2, 16, 48, 128), F32), wide, wide,
-             narrow, narrow, narrow, narrow, narrow, narrow),
+             narrow, narrow, narrow, narrow, narrow, narrow, pltpu.VMEM((512, 256), BF16), pltpu.VMEM((512, 256), BF16)),
         ],
         compiler_params=pltpu.CompilerParams(collective_id=0, has_side_effects=True,
                                              vmem_limit_bytes=53 * 1024 * 1024),

time: 32.2 us -> 30.2 us (0.938)
  Pallas kernels: 31.4 us -> 29.4 us
    pallas_call x1, Pallas kernels: 31.4 us -> 29.4 us  [on_device(): pl.pallas_call(kernel, out_shape=jax.ShapeDtypeStruct((8, 32, 256), F32),...]
where the time goes in v4:
time: 30.2 us; the launch traced here: 30.1 us
  Pallas kernels  29.4 us (97%)
  local copies, waits for them, and re-layouts  0.71 us (2%)
    pallas_call x1, Pallas kernels, on_device(): pl.pallas_call(kernel, out_shape=jax.ShapeDtypeStruct((8, 32, 256), F32),...  29.4 us
    unnamed x1, local copies, waits for them, and re-layouts  0.71 us

profile of v4, /device:TPU:1, one launch (start us, length us, event | category | flops | bytes accessed | tf_op | source)
XLA Modules:
  0.0 30.1 jit_solution(9588798869704162394)
XLA Ops:
  0.0 29.4 %shard_map.28 = f32[8,32,256]{2,1,0:T(8,128)S(1)} custom-call(f32[8]{0:T(128)} %occ_hbm.1, bf16[8,128,16,128]{3,2,1,0:T(8,128)(2,1)} %orb_ref.1), custom_call_target="tpu_custom_call" | custom-call | tf_op jit(solution)/shard_map/pallas_call | solution.py:342
  29.4 0.7 %copy.4 = f32[8,32,256]{2,1,0:T(8,128)} copy(f32[8,32,256]{2,1,0:T(8,128)S(1)} %shard_map.28) | data formatting | bytes 524288

commit v5 on v4

--- a/solution.py
+++ b/solution.py
@@ -14,8 +14,8 @@
 D1, D2, D3, D4 = 224.0, -56.0, 32.0 / 3.0, -1.0
 DERIV = {1: D1, 2: D2, 3: D3, 4: D4}
 
-STEPS = (4, 3, 5, 1, 7, 2, 6, 0)
-FAR = (4, 3, 5, 2, 6)
+STEPS = (4, 3, 2, 1, 5, 6, 7, 0)
+FAR = (4, 3, 2, 5, 6)
 NEAR = (1, 7)
 LAG = 4
 AROUND = tuple((j, e) for j in (1, -1, 0) for e in (1, -1, 0) if (j, e) != (0, 0))
@@ -54,14 +54,15 @@
 
 def build_matrices(wide_w, low_w, deriv_w, weave_w):
     refine = circulant(REFINE).astype(BF16)
-    wide_w[0:128, 0:128] = refine
-    wide_w[128:256, 0:128] = refine
+    for t in (0, 128, 256):
+        wide_w[t:t + 128, 0:128] = refine
     for r in (0, 1):
         high, low = two_terms(circulant(composed(r)))
         columns = slice(128 + 128 * r, 256 + 128 * r)
-        wide_w[0:128, columns] = high
-        wide_w[128:256, columns] = high
-        low_w[:, 128 * r:128 * r + 128] = low
+        for t in (0, 128, 256):
+            wide_w[t:t + 128, columns] = high
+        for t in (0, 128):
+            low_w[t:t + 128, 128 * r:128 * r + 128] = low
     for r in (0, 1):
         source = 2 * lax.broadcasted_iota(jnp.int32, (128, 256), 0) + r
         target = lax.broadcasted_iota(jnp.int32, (128, 256), 1)
@@ -178,7 +179,7 @@
                               z_peer(k), dom))
     build_matrices(*matrices)
     for n, k in enumerate(FAR):
-        if n == 2:
+        if n == 3:
             for copy in to_near:
                 copy.wait_recv()
             from_core[7] = from_core[7] + (from_near[0] + from_near[1])
@@ -264,14 +265,16 @@
 
     def third(*starts):
         cells = jnp.concatenate([fe[:, pl.ds(r0, 16), :].reshape(384, 128) for r0 in starts], axis=0)
-        high, low = two_terms(cells)
-        both = jnp.concatenate([high, low], axis=1)
-        odd = dot(both, wide_w[:, 0:128])
+        high = cells.astype(BF16)
+        middle, low = two_terms(cells - high.astype(F32))
+        terms = jnp.concatenate([high, middle, low], axis=1)
+        odd = dot(terms, wide_w[:, 0:128])
 
         def inner(v):
             return jnp.concatenate([v[384 * i + 64:384 * i + 320] for i in range(len(starts))], axis=0)
 
-        g = dot(inner(both), wide_w[:, 128:384]) + dot(inner(high), low_w[...])
+        kept = inner(terms)
+        g = dot(kept, wide_w[:, 128:384]) + dot(kept[:, 0:256], low_w[...])
         for i, r0 in enumerate(starts):
             rs = pl.ds(r0, 16)
             fo[:, rs, :] = odd[384 * i:384 * i + 384].reshape(24, 16, 128)
@@ -356,7 +359,7 @@
             dma((8,)), dma((8,)), dma((8,)), dma((8,)), dma((8,)), dma((5,)), dma((5,)),
             dma((2,)), dma((2,)), pltpu.SemaphoreType.REGULAR, pltpu.SemaphoreType.REGULAR,
             dma((len(PARTNERS),)), dma((len(PARTNERS),)),
-            (pltpu.VMEM((256, 384), BF16), pltpu.VMEM((128, 256), BF16),
+            (pltpu.VMEM((384, 384), BF16), pltpu.VMEM((256, 256), BF16),
              pltpu.VMEM((256, 256), BF16), pltpu.VMEM((256, 256), BF16)),
             (pltpu.VMEM((24, 32, 128), F32), fine, fine, pltpu.VMEM((2, 16, 48, 128), F32), wide, wide,
              narrow, narrow, narrow, narrow, narrow, narrow, pltpu.VMEM((512, 256), BF16), pltpu.VMEM((512, 256), BF16)),

time: 30.2 us -> 30.4 us (level)
  no operation moved by 1% of the time
where the time goes in v5:
time: 30.4 us; the launch traced here: 30.3 us
  Pallas kernels  29.6 us (97%)
  local copies, waits for them, and re-layouts  0.71 us (2%)
    pallas_call x1, Pallas kernels, on_device(): pl.pallas_call(kernel, out_shape=jax.ShapeDtypeStruct((8, 32, 256), F32),...  29.6 us
    unnamed x1, local copies, waits for them, and re-layouts  0.71 us

profile of v5, /device:TPU:1, one launch (start us, length us, event | category | flops | bytes accessed | tf_op | source)
XLA Modules:
  0.0 30.3 jit_solution(6787966898004084555)
XLA Ops:
  0.0 29.6 %shard_map.28 = f32[8,32,256]{2,1,0:T(8,128)S(1)} custom-call(f32[8]{0:T(128)} %occ_hbm.1, bf16[8,128,16,128]{3,2,1,0:T(8,128)(2,1)} %orb_ref.1), custom_call_target="tpu_custom_call" | custom-call | tf_op jit(solution)/shard_map/pallas_call | solution.py:345
  29.6 0.7 %copy.4 = f32[8,32,256]{2,1,0:T(8,128)} copy(f32[8,32,256]{2,1,0:T(8,128)S(1)} %shard_map.28) | data formatting | bytes 524288
